TPU v7x, 32 devices: a whole 2x2x4 slice. The times are simulated.
32 devices in a mesh: seq: 4 (over y, core), lat: 4 (over z), batch: 2 (over x).
Axes of the slice: x: 2, y: 2, z: 4, core: 2. Of those that a mesh axis runs over, the one named last changes fastest.
Arguments:
- activations: bfloat16 [2, 1024, 3584], P('batch', 'seq'), may hold values from -6 to 6
- dictionary: bfloat16 [4096, 3584], P('lat'), may hold values from -0.09375 to 0.09375
- topk_ids: int32 [2, 1024, 64], P('batch', 'seq'), may hold values from 0 to 4095, as said below
- kernel_taps: float32 [9, 4096], P(None, 'lat'), may hold values from -2 to 2
- enc_bias: float32 [4096], P('lat'), may hold values from -3 to 3
Outputs:
- grad_dictionary: float32 [4096, 3584], P('lat', ('seq', 'batch'))
- grad_taps: float32 [9, 4096], P(None, 'lat')
- grad_bias: float32 [4096], P('lat')
Inputs may be any that keep to these rules, and one draw needn't show every extreme that they name: `topk_ids`: each position names 64 different latents.
All inputs are finite; a program needn't handle non-finite values.
Results may differ from a plain program's by a relative error of at most 0.017.
Values may be sent and summed in bfloat16 or wider, within the bound.
No kernel may reach another device: no remote copies, remote signals or barrier semaphores. Data moves between devices by JAX's collectives and lax.ppermute only.
A program may use at most 128 MiB of HBM per device.

v0:
```python
import jax
import jax.numpy as jnp
from jax import lax
from jax.sharding import PartitionSpec as P

TAPS = 9
HALF = 4


def extended(cells, sides, width):
    for axis, dim in sides:
        count = lax.axis_size(axis)
        ends = count - 1
        head = lax.slice_in_dim(cells, 0, width, axis=dim)
        tail = lax.slice_in_dim(cells, cells.shape[dim] - width, cells.shape[dim], axis=dim)
        cells = jnp.concatenate(
            [
                lax.ppermute(tail, axis, [(i, (i + 1) % count) for i in range(ends)]),
                cells,
                lax.ppermute(head, axis, [((i + 1) % count, i) for i in range(ends)]),
            ],
            axis=dim,
        )
    return cells


def body(activations, dictionary, topk_ids, kernel_taps, enc_bias):
    token_rows = activations[0]
    chosen_ids = topk_ids[0]
    positions = token_rows.shape[0]
    width_local = dictionary.shape[0]
    latent_in = jnp.einsum("td,ld->tl", token_rows, dictionary, preferred_element_type=jnp.float32)
    padded_in = extended(latent_in.astype(jnp.bfloat16), (("seq", 0),), HALF).astype(
        latent_in.dtype
    )
    preact = jnp.zeros(latent_in.shape, jnp.float32)
    for tap_index in range(TAPS):
        preact = (
            preact + kernel_taps[tap_index][None, :] * padded_in[tap_index : tap_index + positions]
        )
    preact = preact + enc_bias[None, :]
    first_latent = lax.axis_index("lat") * width_local
    latent_ids = first_latent + jnp.arange(width_local, dtype=jnp.int32)
    active = jnp.any(chosen_ids[:, :, None] == latent_ids[None, None, :], axis=1).astype(
        jnp.float32
    )
    latents = (active * preact).astype(jnp.bfloat16)
    recon_part = jnp.einsum("tl,ld->td", latents, dictionary, preferred_element_type=jnp.float32)
    recon_full = lax.psum(recon_part.astype(jnp.bfloat16), "lat").astype(jnp.float32)
    error_rows = (recon_full - token_rows.astype(jnp.float32)).astype(jnp.bfloat16)
    grad_code = jnp.einsum("td,ld->tl", error_rows, dictionary, preferred_element_type=jnp.float32)
    decoder_term = jnp.einsum("tl,td->ld", latents, error_rows, preferred_element_type=jnp.float32)
    grad_pre = active * grad_code
    padded_grad = extended(grad_pre.astype(jnp.bfloat16), (("seq", 0),), HALF).astype(
        grad_pre.dtype
    )
    grad_wide = jnp.zeros(grad_pre.shape, jnp.float32)
    for tap_index in range(TAPS):
        begin = 2 * HALF - tap_index
        grad_wide = (
            grad_wide + kernel_taps[tap_index][None, :] * padded_grad[begin : begin + positions]
        )
    grad_in = grad_wide.astype(jnp.bfloat16)
    tap_parts = jnp.stack(
        [
            jnp.sum(grad_pre * padded_in[tap_index : tap_index + positions], axis=0)
            for tap_index in range(TAPS)
        ]
    )
    bias_part = jnp.sum(grad_pre, axis=0)
    grad_taps, grad_bias = (
        lax.psum(tap_parts.astype(jnp.bfloat16), ("seq", "batch")).astype(jnp.float32),
        lax.psum(bias_part.astype(jnp.bfloat16), ("seq", "batch")).astype(jnp.float32),
    )
    dict_term = decoder_term + jnp.einsum(
        "tl,td->ld", grad_in, token_rows, preferred_element_type=jnp.float32
    )
    dict_rounded = lax.optimization_barrier(dict_term.astype(jnp.bfloat16)).astype(jnp.float32)
    grad_dictionary = lax.psum_scatter(
        dict_rounded.astype(jnp.bfloat16), ("seq", "batch"), scatter_dimension=1, tiled=True
    ).astype(jnp.float32)
    return (grad_dictionary, grad_taps, grad_bias)


def solution(mesh):
    return jax.shard_map(
        body,
        mesh=mesh,
        in_specs=(
            P("batch", "seq", None),
            P("lat", None),
            P("batch", "seq", None),
            P(None, "lat"),
            P("lat"),
        ),
        out_specs=(P("lat", ("seq", "batch")), P(None, "lat"), P("lat")),
        check_vma=False,
    )
```

profile of v0, /device:TPU:0, one launch (start us, length us, event | category | flops | bytes accessed | tf_op | source)
XLA Modules:
  0.0 228.1 jit_solution(14252760206919409819)
XLA Ops:
  7.2 5.7 %fusion.3 = bf16[256,1024]{1,0:T(8,128)(2,1)S(1)} fusion(bf16[1024,3584]{1,0:T(8,128)(2,1)} %param.6, bf16[1,256,3584]{2,1,0:T(8,128)(2,1)} %param.5), kind=kOutput, calls=%fused_computation.8 | convolution fusion | flops 1879310336 | bytes 9699328 | tf_op jit(solution)/shard_map/td,ld->tl/dot_general | solution.py:32
  13.0 1.3 collective-permute-start.1
  14.3 3.0 %collective-permute-start = (bf16[4,1024]{1,0:T(4,128)(2,1)S(1)}, bf16[4,1024]{1,0:T(4,128)(2,1)S(1)}, u32[]{:S(2)}, u32[]{:S(2)}) collective-permute-start(bf16[4,1024]{1,0:T(4,128)(2,1)S(1)} %get-tuple-element.27), channel_id=1, source_target_pairs={{0,8},{8,16},{16,24},{1,9},{9,17},{17,25},{2,10},{10,18},{18,26},{... | collective-permute-start | bytes 24584 | tf_op jit(solution)/shard_map/ppermute | solution.py:18
  17.4 0.1 copy.12
  17.5 9.4 %compare_reduce_fusion = pred[256,1024]{1,0:T(8,128)(4,1)S(1)} fusion(s32[1024]{0:T(1024)S(1)} %iota_add_fusion, s32[256,64]{1,0:T(8,128)S(1)} %copy.12), kind=kLoop, calls=%fused_computation | loop fusion | flops 33292288 | bytes 331776 | tf_op jit(solution)/shard_map/reduce_or | solution.py:44
  27.0 0.1 maximum_convert_fusion
  27.2 1.3 select_convert_fusion
  28.5 1.7 copy-done.6
  30.2 3.3 %convolution_convert_fusion = bf16[256,3584]{1,0:T(8,128)(2,1)} fusion(bf16[256,1024]{1,0:T(8,128)(2,1)S(1)} %select_convert_fusion, bf16[1024,3584]{1,0:T(8,128)(2,1)S(1)} %copy-done.6), kind=kOutput, calls=%fused_computation.2 | convolution fusion | flops 1879965696 | bytes 9699328 | tf_op jit(solution)/shard_map/tl,ld->td/dot_general | solution.py:48
  33.6 80.4 %all-reduce.3.cloned.1.call-done = bf16[256,3584]{1,0:T(8,128)(2,1)} async-done(((bf16[256,3584]{1,0:T(8,128)(2,1)}), bf16[256,3584]{1,0:T(8,128)(2,1)}) %all-reduce.3.cloned.1.call-update) | async-done | bytes 1835024 | tf_op jit(solution)/shard_map/psum | solution.py:49
  114.1 6.9 %multiply_reduce_fusion = (bf16[1024]{0:T(1024)(128)(2,1)S(1)}, bf16[1024]{0:T(1024)(128)(2,1)S(1)}, bf16[1024]{0:T(1024)(128)(2,1)S(1)}, bf16[1024]{0:T(1024)(1...) fusion(f32[264,1024]{1,0:T(8,128)S(1)} %maximum_convert_fusion,, ...), kind=kOutput, calls=%fused_computation.27 | convolution fusion | flops 1888212992 | bytes 21254144 | tf_op jit(solution)/shard_map/td,ld->tl/dot_general | solution.py:51
  121.0 1.3 collective-permute-start.3
  122.3 3.2 %collective-permute-start.2 = (bf16[4,1024]{1,0:T(4,128)(2,1)S(1)}, bf16[4,1024]{1,0:T(4,128)(2,1)S(1)}, u32[]{:S(2)}, u32[]{:S(2)}) collective-permute-start(bf16[4,1024]{1,0:T(4,128)(2,1)S(1)} %get-tuple-element.25), channel_id=1, source_target_pairs={{0,8},{8,16},{16,24},{1,9},{9,17},{17,25},{2,10},{10,18},{18,26},{... | collective-permute-start | bytes 24584 | tf_op jit(solution)/shard_map/ppermute | solution.py:18
  125.5 7.4 %fusion.15 = f32[1024,3584]{1,0:T(8,128)} fusion(bf16[256,1024]{1,0:T(8,128)(2,1)S(1)} %select_convert_fusion, bf16[256,3584]{1,0:T(8,128)(2,1)S(1)} %copy-done.1, bf16[1,256,3584]{2,1,0:T(8,128)(2,1)S(1)} %copy-done), kind=kOutput, calls=%fused_computation.37 | convolution fusion | flops 1882718208 | bytes 18874368 | tf_op jit(solution)/shard_map/tl,td->ld/dot_general | solution.py:52
  132.9 0.2 maximum_convert_fusion.1
  133.1 8.7 %add_convert_fusion = bf16[1024,3584]{1,0:T(8,128)(2,1)} fusion(f32[1024,3584]{1,0:T(8,128)} %fusion.15, bf16[1,256,3584]{2,1,0:T(8,128)(2,1)S(1)} %copy-done, f32[264,1024]{1,0:T(8,128)S(1)} %maximum_convert_fusion.1, f32[1024]{0:T(1024)S(1)} %bitcast.47, f32[1024]{0:T(1024)S(1)} %bitcast.49, f32[1024]{0:T(1024)S(1)} %bitcast.35, f32[1024]{0:T(1024)S(1)} %bitcast.37, ...), kind=kOutput, calls=%fused_computation.1 | convolution fusion | flops 1891106816 | bytes 33329152 | tf_op jit(solution)/shard_map/tl,td->ld/dot_general | solution.py:75
  141.7 10.4 %copy.14 = bf16[1024,3584]{0,1:T(8,128)(2,1)} copy(bf16[1024,3584]{1,0:T(8,128)(2,1)} %add_convert_fusion) | data formatting | bytes 14680064
  152.3 0.1 stack.49
  152.4 24.5 %all-reduce = (bf16[9,1024]{1,0:T(8,128)(2,1)S(1)}, bf16[1024]{0:T(1024)(128)(2,1)S(1)}) all-reduce(bf16[9,1024]{1,0:T(8,128)(2,1)S(1)} %stack.49, bf16[1024]{0:T(1024)(128)(2,1)S(1)} %get-tuple-element.21), channel_id=1, replica_groups=mesh['seq'=4,'lat'=4,'batch'=2] {'seq','batch'}, use_global_device_ids=true, to_apply=%region_12.0 | all-reduce | flops 10240 | bytes 40960 | tf_op jit(solution)/shard_map/psum | solution.py:72
  176.9 0.6 convert_element_type.61
  177.5 0.6 convert_element_type.63
  178.1 40.2 %reduce-scatter.4.cloned.1.call-done = bf16[448,1024]{1,0:T(8,128)(2,1)} async-done(((bf16[3584,1024]{1,0:T(8,128)(2,1)}), bf16[448,1024]{1,0:T(8,128)(2,1)}) %reduce-scatter.4.cloned.1.call-update) | async-done | bytes 917520
  218.3 1.5 copy.15
  219.8 1.5 copy.13
  (34 shorter events, 0.3 us)
Async XLA Ops:
  7.2 10.2 %copy-start.3 = (s32[1,256,64]{1,2,0:T(8,128)S(1)}, s32[1,256,64]{1,2,0:T(8,128)}, u32[]{:S(2)}) copy-start(s32[1,256,64]{1,2,0:T(8,128)} %param.7) | copy-start | bytes 196612
  7.2 19.7 %copy-start.4 = (f32[9,1024]{1,0:T(8,128)S(1)}, f32[9,1024]{1,0:T(8,128)}, u32[]{:S(2)}) copy-start(f32[9,1024]{1,0:T(8,128)} %param.8) | copy-start | bytes 110596
  7.2 106.9 %all-reduce.3.cloned.1.call-start = ((), (), s32[]{:S(2)}) async-start(), calls=%async_computation.1 | async-start | bytes 3670016 | tf_op jit(solution)/shard_map/psum | solution.py:49
  13.0 14.2 %copy-start.5 = (f32[1024]{0:T(1024)S(1)}, f32[1024]{0:T(1024)}, u32[]{:S(2)}) copy-start(f32[1024]{0:T(1024)} %param.9) | copy-start | bytes 12292
  13.0 14.0 %collective-permute-start.1 = (bf16[4,1024]{1,0:T(4,128)(2,1)S(1)}, bf16[4,1024]{1,0:T(4,128)(2,1)S(1)}, u32[]{:S(2)}, u32[]{:S(2)}) collective-permute-start(bf16[4,1024]{1,0:T(4,128)(2,1)S(1)} %get-tuple-element.28), channel_id=1, source_target_pairs={{8,0},{16,8},{24,16},{9,1},{17,9},{25,17},{10,2},{18,10},{26,18},{... | collective-permute-start | bytes 24584 | tf_op jit(solution)/shard_map/ppermute | solution.py:20
  14.3 12.7 %collective-permute-start = (bf16[4,1024]{1,0:T(4,128)(2,1)S(1)}, bf16[4,1024]{1,0:T(4,128)(2,1)S(1)}, u32[]{:S(2)}, u32[]{:S(2)}) collective-permute-start(bf16[4,1024]{1,0:T(4,128)(2,1)S(1)} %get-tuple-element.27), channel_id=1, source_target_pairs={{0,8},{8,16},{16,24},{1,9},{9,17},{17,25},{2,10},{10,18},{18,26},{... | collective-permute-start | bytes 24584 | tf_op jit(solution)/shard_map/ppermute | solution.py:18
  26.9 1.6 copy-start.2
  27.1 3.1 %copy-start.6 = (bf16[1024,3584]{1,0:T(8,128)(2,1)S(1)}, bf16[1024,3584]{1,0:T(8,128)(2,1)}, u32[]{:S(2)}) copy-start(bf16[1024,3584]{1,0:T(8,128)(2,1)} %param.6) | copy-start | bytes 22020100
  33.5 80.5 %copy-start = (bf16[1,256,3584]{2,1,0:T(8,128)(2,1)S(1)}, bf16[1,256,3584]{2,1,0:T(8,128)(2,1)}, u32[]{:S(2)}) copy-start(bf16[1,256,3584]{2,1,0:T(8,128)(2,1)} %param.5) | copy-start | bytes 5505028
  33.6 184.7 %reduce-scatter.4.cloned.1.call-start = ((), (), s32[]{:S(2)}) async-start(), calls=%async_computation.2 | async-start | bytes 8257536
  114.1 11.5 %copy-start.1 = (bf16[256,3584]{1,0:T(8,128)(2,1)S(1)}, bf16[256,3584]{1,0:T(8,128)(2,1)}, u32[]{:S(2)}) copy-start(bf16[256,3584]{1,0:T(8,128)(2,1)} %all-reduce.3.cloned.1.call-done) | copy-start | bytes 5505028
  121.0 11.9 %collective-permute-start.3 = (bf16[4,1024]{1,0:T(4,128)(2,1)S(1)}, bf16[4,1024]{1,0:T(4,128)(2,1)S(1)}, u32[]{:S(2)}, u32[]{:S(2)}) collective-permute-start(bf16[4,1024]{1,0:T(4,128)(2,1)S(1)} %get-tuple-element.26), channel_id=1, source_target_pairs={{8,0},{16,8},{24,16},{9,1},{17,9},{25,17},{10,2},{18,10},{26,18},{... | collective-permute-start | bytes 24584 | tf_op jit(solution)/shard_map/ppermute | solution.py:20
  122.3 10.6 %collective-permute-start.2 = (bf16[4,1024]{1,0:T(4,128)(2,1)S(1)}, bf16[4,1024]{1,0:T(4,128)(2,1)S(1)}, u32[]{:S(2)}, u32[]{:S(2)}) collective-permute-start(bf16[4,1024]{1,0:T(4,128)(2,1)S(1)} %get-tuple-element.25), channel_id=1, source_target_pairs={{0,8},{8,16},{16,24},{1,9},{9,17},{17,25},{2,10},{10,18},{18,26},{... | collective-permute-start | bytes 24584 | tf_op jit(solution)/shard_map/ppermute | solution.py:18
Sparse Core Ops, SparseCore 0:
  33.7 80.3 all-reduce.2
  152.3 65.9 reduce-scatter.3
where the time goes:
time: 229 us; the launch traced here: 228 us
  waiting for transfers between devices  121 us (53%)
  matrix products  32 us (14%)
  blocking collectives  24.5 us (11%)
  local copies, waits for them, and re-layouts  15.4 us (7%)
  between operations  14.3 us (6%)
  other arithmetic  12.3 us (5%)
  starting transfers between devices  8.9 us (4%)
    psum x1, waiting for transfers between devices, body(): lax.psum(recon_part.astype(jnp.bfloat16), 'lat').astype(jnp.float32)  80.4 us
    unnamed x3, waiting for transfers between devices  40.2 us
    psum x1, blocking collectives, body(): lax.psum(tap_parts.astype(jnp.bfloat16), ('seq', 'batch'))  24.5 us
    unnamed x17, local copies, waits for them, and re-layouts  15.1 us
    reduce_or x1, other arithmetic, body(): jnp.any(chosen_ids[:, :, None] == latent_ids[None, None, :], axis=1)  9.43 us
    dot_general x1, matrix products, body(): jnp.einsum('tl,td->ld', grad_in, token_rows, preferred_element_type=jnp.f...  8.66 us
    dot_general x1, matrix products, body(): jnp.einsum('tl,td->ld', latents, error_rows, preferred_element_type=jnp.f...  7.39 us
    dot_general x1, matrix products, body(): jnp.einsum('td,ld->tl', error_rows, dictionary, preferred_element_type=jn...  6.93 us
  transfers between devices with their start and end apart: 6, of which 2 were waited for; matrix products, arithmetic and copies ran while one was open for 8% of the time, Pallas kernels for 0%

commit v1 on v0

--- a/solution.py
+++ b/solution.py
@@ -69,7 +69,7 @@
     )
     bias_part = jnp.sum(grad_pre, axis=0)
     grad_taps, grad_bias = (
-        lax.psum(tap_parts.astype(jnp.bfloat16), ("seq", "batch")).astype(jnp.float32),
+        lax.psum(lax.psum(tap_parts.astype(jnp.bfloat16), "seq"), "batch").astype(jnp.float32),
         lax.psum(bias_part.astype(jnp.bfloat16), ("seq", "batch")).astype(jnp.float32),
     )
     dict_term = decoder_term + jnp.einsum(

time: 229 us -> 229 us (level)
  blocking collectives: 24.5 us -> 32.7 us
  waiting for transfers between devices: 121 us -> 113 us
    psum x1 -> x3, blocking collectives: 24.5 us -> 32.7 us  [the longest x1 13.1 us: body(): lax.psum(bias_part.astype(jnp.bfloat16), ('seq', 'batch'))]
    unnamed x3, waiting for transfers between devices: 40.2 us -> 32.4 us
where the time goes in v1:
time: 229 us
  waiting for transfers between devices  113 us (49%)
  blocking collectives  32.7 us (14%)
  matrix products  32 us (14%)
  local copies, waits for them, and re-layouts  15.4 us (7%)
  between operations  14.3 us (6%)
  other arithmetic  12.3 us (5%)
  starting transfers between devices  8.9 us (4%)
    psum x1, waiting for transfers between devices, body(): lax.psum(recon_part.astype(jnp.bfloat16), 'lat').astype(jnp.float32)  80.4 us
    unnamed x3, waiting for transfers between devices  32.4 us
    unnamed x17, local copies, waits for them, and re-layouts  15.1 us
    psum x1, blocking collectives, body(): lax.psum(bias_part.astype(jnp.bfloat16), ('seq', 'batch'))  13.1 us
    psum x1, blocking collectives, body(): lax.psum(tap_parts.astype(jnp.bfloat16), 'seq')  11.3 us
    reduce_or x1, other arithmetic, body(): jnp.any(chosen_ids[:, :, None] == latent_ids[None, None, :], axis=1)  9.43 us
    dot_general x1, matrix products, body(): jnp.einsum('tl,td->ld', grad_in, token_rows, preferred_element_type=jnp.f...  8.66 us
    psum x1, blocking collectives, body(): lax.psum(lax.psum(tap_parts.astype(jnp.bfloat16), 'seq'), 'batch')  8.32 us
  transfers between devices with their start and end apart: 6, of which 2 were waited for; matrix products, arithmetic and copies ran while one was open for 8% of the time, Pallas kernels for 0%

profile of v1, /device:TPU:0, one launch (start us, length us, event | category | flops | bytes accessed | tf_op | source)
XLA Modules:
  0.0 228.5 jit_solution(8569332942394585748)
XLA Ops:
  7.2 5.7 %fusion.3 = bf16[256,1024]{1,0:T(8,128)(2,1)S(1)} fusion(bf16[1024,3584]{1,0:T(8,128)(2,1)} %param.6, bf16[1,256,3584]{2,1,0:T(8,128)(2,1)} %param.5), kind=kOutput, calls=%fused_computation.8 | convolution fusion | flops 1879310336 | bytes 9699328 | tf_op jit(solution)/shard_map/td,ld->tl/dot_general | solution.py:32
  13.0 1.3 collective-permute-start.1
  14.3 3.0 %collective-permute-start = (bf16[4,1024]{1,0:T(4,128)(2,1)S(1)}, bf16[4,1024]{1,0:T(4,128)(2,1)S(1)}, u32[]{:S(2)}, u32[]{:S(2)}) collective-permute-start(bf16[4,1024]{1,0:T(4,128)(2,1)S(1)} %get-tuple-element.25), channel_id=1, source_target_pairs={{0,8},{8,16},{16,24},{1,9},{9,17},{17,25},{2,10},{10,18},{18,26},{... | collective-permute-start | bytes 24584 | tf_op jit(solution)/shard_map/ppermute | solution.py:18
  17.5 9.4 %compare_reduce_fusion = pred[256,1024]{1,0:T(8,128)(4,1)S(1)} fusion(s32[1024]{0:T(1024)S(1)} %iota_add_fusion, s32[256,64]{1,0:T(8,128)S(1)} %copy.12), kind=kLoop, calls=%fused_computation | loop fusion | flops 33292288 | bytes 331776 | tf_op jit(solution)/shard_map/reduce_or | solution.py:44
  27.0 0.1 maximum_convert_fusion
  27.2 1.3 select_convert_fusion
  28.5 1.7 copy-done.6
  30.2 3.3 %convolution_convert_fusion = bf16[256,3584]{1,0:T(8,128)(2,1)} fusion(bf16[256,1024]{1,0:T(8,128)(2,1)S(1)} %select_convert_fusion, bf16[1024,3584]{1,0:T(8,128)(2,1)S(1)} %copy-done.6), kind=kOutput, calls=%fused_computation.2 | convolution fusion | flops 1879965696 | bytes 9699328 | tf_op jit(solution)/shard_map/tl,ld->td/dot_general | solution.py:48
  33.6 80.4 %all-reduce.2.cloned.1.call-done = bf16[256,3584]{1,0:T(8,128)(2,1)} async-done(((bf16[256,3584]{1,0:T(8,128)(2,1)}), bf16[256,3584]{1,0:T(8,128)(2,1)}) %all-reduce.2.cloned.1.call-update) | async-done | bytes 1835024 | tf_op jit(solution)/shard_map/psum | solution.py:49
  114.1 6.9 %multiply_reduce_fusion = (bf16[1024]{0:T(1024)(128)(2,1)S(1)}, bf16[1024]{0:T(1024)(128)(2,1)S(1)}, bf16[1024]{0:T(1024)(128)(2,1)S(1)}, bf16[1024]{0:T(1024)(1...) fusion(f32[264,1024]{1,0:T(8,128)S(1)} %maximum_convert_fusion,, ...), kind=kOutput, calls=%fused_computation.27 | convolution fusion | flops 1888212992 | bytes 21254144 | tf_op jit(solution)/shard_map/td,ld->tl/dot_general | solution.py:51
  121.0 1.3 collective-permute-start.3
  122.3 3.2 %collective-permute-start.2 = (bf16[4,1024]{1,0:T(4,128)(2,1)S(1)}, bf16[4,1024]{1,0:T(4,128)(2,1)S(1)}, u32[]{:S(2)}, u32[]{:S(2)}) collective-permute-start(bf16[4,1024]{1,0:T(4,128)(2,1)S(1)} %get-tuple-element.23), channel_id=1, source_target_pairs={{0,8},{8,16},{16,24},{1,9},{9,17},{17,25},{2,10},{10,18},{18,26},{... | collective-permute-start | bytes 24584 | tf_op jit(solution)/shard_map/ppermute | solution.py:18
  125.5 7.4 %fusion.15 = f32[1024,3584]{1,0:T(8,128)} fusion(bf16[256,1024]{1,0:T(8,128)(2,1)S(1)} %select_convert_fusion, bf16[256,3584]{1,0:T(8,128)(2,1)S(1)} %copy-done.1, bf16[1,256,3584]{2,1,0:T(8,128)(2,1)S(1)} %copy-done), kind=kOutput, calls=%fused_computation.37 | convolution fusion | flops 1882718208 | bytes 18874368 | tf_op jit(solution)/shard_map/tl,td->ld/dot_general | solution.py:52
  132.9 0.2 maximum_convert_fusion.1
  133.1 8.7 %add_convert_fusion = bf16[1024,3584]{1,0:T(8,128)(2,1)} fusion(f32[1024,3584]{1,0:T(8,128)} %fusion.15, bf16[1,256,3584]{2,1,0:T(8,128)(2,1)S(1)} %copy-done, f32[264,1024]{1,0:T(8,128)S(1)} %maximum_convert_fusion.1, f32[1024]{0:T(1024)S(1)} %bitcast.47, f32[1024]{0:T(1024)S(1)} %bitcast.49, f32[1024]{0:T(1024)S(1)} %bitcast.35, f32[1024]{0:T(1024)S(1)} %bitcast.37, ...), kind=kOutput, calls=%fused_computation.1 | convolution fusion | flops 1891106816 | bytes 33329152 | tf_op jit(solution)/shard_map/tl,td->ld/dot_general | solution.py:75
  141.7 10.4 %copy.14 = bf16[1024,3584]{0,1:T(8,128)(2,1)} copy(bf16[1024,3584]{1,0:T(8,128)(2,1)} %add_convert_fusion) | data formatting | bytes 14680064
  152.4 11.3 %psum.29 = bf16[9,1024]{1,0:T(8,128)(2,1)S(1)} all-reduce(bf16[9,1024]{1,0:T(8,128)(2,1)S(1)} %stack.49), channel_id=1, replica_groups=mesh['seq'=4,'lat'=4,'batch'=2] {'seq'}, use_global_device_ids=true, to_apply=%region_12.0 | all-reduce | flops 9216 | bytes 36864 | tf_op jit(solution)/shard_map/psum | solution.py:72
  163.7 8.3 %psum.30 = bf16[9,1024]{1,0:T(8,128)(2,1)S(1)} all-reduce(bf16[9,1024]{1,0:T(8,128)(2,1)S(1)} %psum.29), channel_id=1, replica_groups=mesh['seq'=4,'lat'=4,'batch'=2] {'batch'}, use_global_device_ids=true, to_apply=%region_13.0 | all-reduce | flops 9216 | bytes 36864 | tf_op jit(solution)/shard_map/psum | solution.py:72
  172.0 0.6 convert_element_type.61
  172.7 13.1 %psum.31 = bf16[1024]{0:T(1024)(128)(2,1)S(1)} all-reduce(bf16[1024]{0:T(1024)(128)(2,1)S(1)} %get-tuple-element.21), channel_id=1, replica_groups=mesh['seq'=4,'lat'=4,'batch'=2] {'seq','batch'}, use_global_device_ids=true, to_apply=%region_15.0 | all-reduce | flops 1024 | bytes 4096 | tf_op jit(solution)/shard_map/psum | solution.py:73
  185.8 0.6 convert_element_type.63
  186.4 32.4 %reduce-scatter.4.cloned.1.call-done = bf16[448,1024]{1,0:T(8,128)(2,1)} async-done(((bf16[3584,1024]{1,0:T(8,128)(2,1)}), bf16[448,1024]{1,0:T(8,128)(2,1)}) %reduce-scatter.4.cloned.1.call-update) | async-done | bytes 917520
  218.7 1.5 copy.15
  220.2 1.5 copy.13
  (36 shorter events, 0.4 us)
Async XLA Ops:
  7.2 10.2 %copy-start.3 = (s32[1,256,64]{1,2,0:T(8,128)S(1)}, s32[1,256,64]{1,2,0:T(8,128)}, u32[]{:S(2)}) copy-start(s32[1,256,64]{1,2,0:T(8,128)} %param.7) | copy-start | bytes 196612
  7.2 19.7 %copy-start.4 = (f32[9,1024]{1,0:T(8,128)S(1)}, f32[9,1024]{1,0:T(8,128)}, u32[]{:S(2)}) copy-start(f32[9,1024]{1,0:T(8,128)} %param.8) | copy-start | bytes 110596
  7.2 106.9 %all-reduce.2.cloned.1.call-start = ((), (), s32[]{:S(2)}) async-start(), calls=%async_computation.1 | async-start | bytes 3670016 | tf_op jit(solution)/shard_map/psum | solution.py:49
  13.0 14.2 %copy-start.5 = (f32[1024]{0:T(1024)S(1)}, f32[1024]{0:T(1024)}, u32[]{:S(2)}) copy-start(f32[1024]{0:T(1024)} %param.9) | copy-start | bytes 12292
  13.0 14.0 %collective-permute-start.1 = (bf16[4,1024]{1,0:T(4,128)(2,1)S(1)}, bf16[4,1024]{1,0:T(4,128)(2,1)S(1)}, u32[]{:S(2)}, u32[]{:S(2)}) collective-permute-start(bf16[4,1024]{1,0:T(4,128)(2,1)S(1)} %get-tuple-element.26), channel_id=1, source_target_pairs={{8,0},{16,8},{24,16},{9,1},{17,9},{25,17},{10,2},{18,10},{26,18},{... | collective-permute-start | bytes 24584 | tf_op jit(solution)/shard_map/ppermute | solution.py:20
  14.3 12.7 %collective-permute-start = (bf16[4,1024]{1,0:T(4,128)(2,1)S(1)}, bf16[4,1024]{1,0:T(4,128)(2,1)S(1)}, u32[]{:S(2)}, u32[]{:S(2)}) collective-permute-start(bf16[4,1024]{1,0:T(4,128)(2,1)S(1)} %get-tuple-element.25), channel_id=1, source_target_pairs={{0,8},{8,16},{16,24},{1,9},{9,17},{17,25},{2,10},{10,18},{18,26},{... | collective-permute-start | bytes 24584 | tf_op jit(solution)/shard_map/ppermute | solution.py:18
  26.9 1.6 copy-start.2
  27.1 3.1 %copy-start.6 = (bf16[1024,3584]{1,0:T(8,128)(2,1)S(1)}, bf16[1024,3584]{1,0:T(8,128)(2,1)}, u32[]{:S(2)}) copy-start(bf16[1024,3584]{1,0:T(8,128)(2,1)} %param.6) | copy-start | bytes 22020100
  33.5 80.5 %copy-start = (bf16[1,256,3584]{2,1,0:T(8,128)(2,1)S(1)}, bf16[1,256,3584]{2,1,0:T(8,128)(2,1)}, u32[]{:S(2)}) copy-start(bf16[1,256,3584]{2,1,0:T(8,128)(2,1)} %param.5) | copy-start | bytes 5505028
  33.6 185.2 %reduce-scatter.4.cloned.1.call-start = ((), (), s32[]{:S(2)}) async-start(), calls=%async_computation.2 | async-start | bytes 8257536
  114.1 11.5 %copy-start.1 = (bf16[256,3584]{1,0:T(8,128)(2,1)S(1)}, bf16[256,3584]{1,0:T(8,128)(2,1)}, u32[]{:S(2)}) copy-start(bf16[256,3584]{1,0:T(8,128)(2,1)} %all-reduce.2.cloned.1.call-done) | copy-start | bytes 5505028
  121.0 11.9 %collective-permute-start.3 = (bf16[4,1024]{1,0:T(4,128)(2,1)S(1)}, bf16[4,1024]{1,0:T(4,128)(2,1)S(1)}, u32[]{:S(2)}, u32[]{:S(2)}) collective-permute-start(bf16[4,1024]{1,0:T(4,128)(2,1)S(1)} %get-tuple-element.24), channel_id=1, source_target_pairs={{8,0},{16,8},{24,16},{9,1},{17,9},{25,17},{10,2},{18,10},{26,18},{... | collective-permute-start | bytes 24584 | tf_op jit(solution)/shard_map/ppermute | solution.py:20
  122.3 10.6 %collective-permute-start.2 = (bf16[4,1024]{1,0:T(4,128)(2,1)S(1)}, bf16[4,1024]{1,0:T(4,128)(2,1)S(1)}, u32[]{:S(2)}, u32[]{:S(2)}) collective-permute-start(bf16[4,1024]{1,0:T(4,128)(2,1)S(1)} %get-tuple-element.23), channel_id=1, source_target_pairs={{0,8},{8,16},{16,24},{1,9},{9,17},{17,25},{2,10},{10,18},{18,26},{... | collective-permute-start | bytes 24584 | tf_op jit(solution)/shard_map/ppermute | solution.py:18
Sparse Core Ops, SparseCore 0:
  33.7 80.3 all-reduce.1
  152.3 66.3 reduce-scatter.3
